TPU v7x, 32 devices: a whole 2x2x4 slice. The times are simulated.
32 devices in a mesh: dp: 8 (over z, y), mp: 4 (over x, core).
Axes of the slice: x: 2, y: 2, z: 4, core: 2. Of those that a mesh axis runs over, the one named last changes fastest.
Arguments:
- queries: bfloat16 [128, 8192], P('dp', 'mp'), may hold values from -8 to 8
- incoming_key: bfloat16 [128, 1024], P('dp', 'mp'), may hold values from -4 to 4
- incoming_value: bfloat16 [128, 1024], P('dp', 'mp'), may hold values from -4 to 4
- key_cache: bfloat16 [256, 256, 1024], P('dp', None, 'mp'), may hold values from -8 to 8
- cached_values: bfloat16 [256, 256, 1024], P('dp', None, 'mp'), may hold values from -4 to 4
- task_key_scale: bfloat16 [256, 1024], P(None, 'mp'), may hold values from 0.099609375 to 1.8984375
- task_value_scale: bfloat16 [256, 1024], P(None, 'mp'), may hold values from 0.099609375 to 1.8984375
- out_weight: bfloat16 [8192, 8192], P('mp', 'dp'), may hold values from -0.0625 to 0.0625
- task_id: int32 [128], P('dp'), may hold values from 0 to 255, as said below
- cached_length: int32 [128], P('dp'), may hold values from 1 to 256, as said below
- task_owner: int32 [256], replicated, may hold values from 0 to 7, as said below
- cache_slot: int32 [128], P('dp'), may hold values from 0 to 31, as said below
Outputs:
- layer_out: bfloat16 [128, 8192], P('dp', 'mp')
Inputs may be any that keep to these rules, and one draw needn't show every extreme that they name: `task_owner`: every dp index owns the same number of tasks. `task_id`: among the 16 requests of one dp index at most 4 have tasks of one owner; in every draw one owner gets exactly 4 from every dp index. `cache_slot`: requests of one owner have distinct slots; one owner uses all 32. `cached_length`: every dp index has a request with 256 cached positions.
All inputs are finite; a program needn't handle non-finite values.
Results may differ from a plain program's by a relative error of at most 0.0073.
Values may be sent and summed in bfloat16 or wider, within the bound.
A program may use at most 128 MiB of HBM per device.

v0:
```python
import math
import jax
import jax.numpy as jnp
from jax import lax
from jax.sharding import PartitionSpec as P

KEY_VALUE_HEADS = 8
HEAD_SIZE = 128
QUERY_HEADS = 64
MAX_POSITIONS = 256
masked_score = -1e30


def attend(queries, fresh_key_rows, fresh_value_rows, stored_key_rows, stored_value_rows, lengths):
    entry_count = queries.shape[0]
    kv_heads = fresh_key_rows.shape[1] // HEAD_SIZE
    group_width = QUERY_HEADS // KEY_VALUE_HEADS
    inv_root = 1.0 / math.sqrt(HEAD_SIZE)
    query_head_rows = queries.reshape(entry_count, kv_heads, group_width, HEAD_SIZE)
    previous_keys = stored_key_rows.reshape(entry_count, MAX_POSITIONS, kv_heads, HEAD_SIZE)
    previous_values = stored_value_rows.reshape(entry_count, MAX_POSITIONS, kv_heads, HEAD_SIZE)
    incoming_keys = fresh_key_rows.reshape(entry_count, kv_heads, HEAD_SIZE)
    incoming_values = fresh_value_rows.reshape(entry_count, kv_heads, HEAD_SIZE)
    scores = (
        jnp.einsum(
            "ngqd,njgd->ngqj", query_head_rows, previous_keys, preferred_element_type=jnp.float32
        )
        * inv_root
    )
    own_score = (
        jnp.einsum(
            "ngqd,ngd->ngq", query_head_rows, incoming_keys, preferred_element_type=jnp.float32
        )
        * inv_root
    )
    visible = (
        lax.broadcasted_iota(jnp.int32, (entry_count, 1, 1, MAX_POSITIONS), 3)
        < lengths[:, None, None, None]
    )
    scores = jnp.where(visible, scores, masked_score)
    top_score = jnp.maximum(jnp.max(scores, axis=3), own_score)
    weights = jnp.where(visible, jnp.exp(scores - top_score[..., None]), 0.0)
    own_weight = jnp.exp(own_score - top_score)
    weight_sum = jnp.sum(weights, axis=3) + own_weight
    blended = jnp.einsum(
        "ngqj,njgd->ngqd",
        weights.astype(jnp.bfloat16),
        previous_values,
        preferred_element_type=jnp.float32,
    )
    blended = (
        blended
        + own_weight.astype(jnp.bfloat16).astype(jnp.float32)[..., None]
        * incoming_values.astype(jnp.float32)[:, :, None, :]
    )
    return (
        (blended / weight_sum[..., None])
        .astype(jnp.bfloat16)
        .reshape(entry_count, kv_heads * group_width * HEAD_SIZE)
    )


def on_device(
    queries,
    incoming_key,
    incoming_value,
    key_cache,
    cached_values,
    task_key_scale,
    task_value_scale,
    out_weight,
    task_id,
    cached_length,
    task_owner,
    cache_slot,
):
    row_count = queries.shape[0]
    task_count = task_key_scale.shape[0]
    kv_width = incoming_key.shape[1]
    kv_heads = kv_width // HEAD_SIZE
    group_width = QUERY_HEADS // KEY_VALUE_HEADS
    owner_count = lax.axis_size("dp")
    capacity = 2 * row_count // owner_count
    picked = task_id[:, None] == lax.broadcasted_iota(jnp.int32, (row_count, task_count), 1)
    owner_of = jnp.sum(jnp.where(picked, task_owner[None, :], 0), axis=1)
    selector = picked.astype(jnp.bfloat16)
    key_factor = jnp.dot(selector, task_key_scale, preferred_element_type=jnp.float32)
    value_factor = jnp.dot(selector, task_value_scale, preferred_element_type=jnp.float32)
    scaled_rows = (
        (
            queries.astype(jnp.float32).reshape(row_count, kv_heads, group_width, HEAD_SIZE)
            * key_factor.reshape(row_count, kv_heads, 1, HEAD_SIZE)
        )
        .astype(jnp.bfloat16)
        .reshape(row_count, kv_heads * group_width * HEAD_SIZE)
    )
    head_width = scaled_rows.shape[1]
    earlier = lax.broadcasted_iota(jnp.int32, (row_count, row_count), 1) < lax.broadcasted_iota(
        jnp.int32, (row_count, row_count), 0
    )
    same_owner = owner_of[:, None] == owner_of[None, :]
    rank_in = jnp.sum(jnp.where(earlier & same_owner, 1, 0), axis=1)
    position = owner_of * capacity + rank_in
    slot_total = owner_count * capacity
    placing = position[None, :] == lax.broadcasted_iota(jnp.int32, (slot_total, row_count), 0)
    packer = placing.astype(jnp.bfloat16)
    unpacker = (
        position[:, None] == lax.broadcasted_iota(jnp.int32, (row_count, slot_total), 1)
    ).astype(jnp.bfloat16)

    def pack_rows(value_rows):
        packed = jnp.dot(packer, value_rows, preferred_element_type=jnp.float32).astype(
            jnp.bfloat16
        )
        return packed.reshape(owner_count, capacity, value_rows.shape[1])

    def pack_ints(value_rows):
        return (
            jnp.sum(jnp.where(placing, value_rows[None, :] + 1, 0), axis=1).reshape(
                owner_count, capacity
            )
            - 1
        )

    got_queries = lax.all_to_all(
        pack_rows(scaled_rows), "dp", split_axis=0, concat_axis=0, tiled=True
    )
    got_keys = lax.all_to_all(
        pack_rows(incoming_key), "dp", split_axis=0, concat_axis=0, tiled=True
    )
    got_values = lax.all_to_all(
        pack_rows(incoming_value), "dp", split_axis=0, concat_axis=0, tiled=True
    )
    slot_ids = lax.all_to_all(pack_ints(cache_slot), "dp", split_axis=0, concat_axis=0, tiled=True)
    got_lengths = lax.all_to_all(
        pack_ints(cached_length), "dp", split_axis=0, concat_axis=0, tiled=True
    )
    sources = slot_ids.shape[0]
    per_source = slot_ids.shape[1]
    item_total = sources * per_source
    flat_slots = jnp.maximum(slot_ids.reshape(item_total), 0)
    stored_key_rows = jnp.take(key_cache, flat_slots, axis=0)
    stored_value_rows = jnp.take(cached_values, flat_slots, axis=0)
    result = attend(
        got_queries.reshape(item_total, head_width),
        got_keys.reshape(item_total, kv_width),
        got_values.reshape(item_total, kv_width),
        stored_key_rows,
        stored_value_rows,
        got_lengths.reshape(item_total),
    )
    answered = result.reshape(sources, per_source, head_width)
    returned = lax.all_to_all(answered, "dp", split_axis=0, concat_axis=0, tiled=True)
    attention_output = jnp.dot(
        unpacker, returned.reshape(slot_total, head_width), preferred_element_type=jnp.float32
    ).astype(jnp.bfloat16)
    context_rows = (
        (
            attention_output.astype(jnp.float32).reshape(
                row_count, kv_heads, group_width, HEAD_SIZE
            )
            * value_factor.reshape(row_count, kv_heads, 1, HEAD_SIZE)
        )
        .astype(jnp.bfloat16)
        .reshape(row_count, head_width)
    )
    all_rows = lax.all_gather(context_rows, "dp", axis=0, tiled=True)
    partial_value = jnp.dot(all_rows, out_weight, preferred_element_type=jnp.float32).astype(
        jnp.bfloat16
    )
    own_rows = lax.all_to_all(partial_value, "dp", split_axis=0, concat_axis=1, tiled=True)
    return lax.psum_scatter(
        own_rows.astype(jnp.float32), "mp", scatter_dimension=1, tiled=True
    ).astype(jnp.bfloat16)


def solution(mesh):
    placed = (
        P("dp", "mp"),
        P("dp", "mp"),
        P("dp", "mp"),
        P("dp", None, "mp"),
        P("dp", None, "mp"),
        P(None, "mp"),
        P(None, "mp"),
        P("mp", "dp"),
        P("dp"),
        P("dp"),
        P(),
        P("dp"),
    )
    return jax.shard_map(
        on_device, mesh=mesh, in_specs=placed, out_specs=P("dp", "mp"), check_vma=False
    )
```

profile of v0, /device:TPU:0, one launch (start us, length us, event | category | flops | bytes accessed | tf_op | source)
XLA Modules:
  0.0 166.6 jit_solution(14488211424720832008)
XLA Ops:
  6.5 0.9 select_reduce_fusion
  9.7 7.3 %all-to-all-start.2 = ((s32[8,1,4]{2,1,0:T(1,128)}), s32[8,1,4]{2,1,0:T(1,128)S(1)}, u32[]{:S(2)}, u32[]{:S(2)}) async-start(s32[8,1,4]{2,1,0:T(1,128)} %bitcast.1), calls=%async_computation.2 | async-start | bytes 8192 | tf_op jit(solution)/shard_map/all_to_all | solution.py:134
  17.0 0.8 fusion.33
  17.9 1.0 convolution_convert_fusion.4
  18.9 1.0 convolution_convert_fusion.3
  19.8 1.1 convolution_convert_fusion
  23.6 6.0 %all-to-all-start = ((s32[8,1,4]{2,1,0:T(1,128)}), s32[8,1,4]{2,1,0:T(1,128)S(1)}, u32[]{:S(2)}, u32[]{:S(2)}) async-start(s32[8,1,4]{2,1,0:T(1,128)} %bitcast), calls=%async_computation | async-start | bytes 8192 | tf_op jit(solution)/shard_map/all_to_all | solution.py:135
  29.7 6.4 %all-to-all-done = s32[8,1,4]{2,1,0:T(1,128)S(1)} async-done(((s32[8,1,4]{2,1,0:T(1,128)}), s32[8,1,4]{2,1,0:T(1,128)S(1)}, u32[]{:S(2)}, u32[]{:S(2)}) %all-to-all-start) | async-done | bytes 160 | tf_op jit(solution)/shard_map/all_to_all | solution.py:135
  36.1 3.3 %all-to-all-start.3 = ((bf16[8,4,256]{2,1,0:T(4,128)(2,1)}), bf16[8,4,256]{2,1,0:T(4,128)(2,1)S(1)}, u32[]{:S(2)}, u32[]{:S(2)}) async-start(bf16[8,4,256]{2,1,0:T(4,128)(2,1)} %reshape.126), calls=%async_computation.3 | async-start | bytes 32768 | tf_op jit(solution)/shard_map/all_to_all | solution.py:128
  39.4 6.5 %all-to-all-done.3 = bf16[8,4,256]{2,1,0:T(4,128)(2,1)S(1)} async-done(((bf16[8,4,256]{2,1,0:T(4,128)(2,1)}), bf16[8,4,256]{2,1,0:T(4,128)(2,1)S(1)}, u32[]{:S(2)}, u32[]{:S(2)}) %all-to-all-start.3) | async-done | bytes 16416 | tf_op jit(solution)/shard_map/all_to_all | solution.py:128
  45.9 3.3 %all-to-all-start.4 = ((bf16[8,4,256]{2,1,0:T(4,128)(2,1)}), bf16[8,4,256]{2,1,0:T(4,128)(2,1)S(1)}, u32[]{:S(2)}, u32[]{:S(2)}) async-start(bf16[8,4,256]{2,1,0:T(4,128)(2,1)} %reshape.128), calls=%async_computation.4 | async-start | bytes 32768 | tf_op jit(solution)/shard_map/all_to_all | solution.py:131
  49.2 4.9 %gather_fusion = bf16[32,256,256]{2,1,0:T(8,128)(2,1)} fusion(bf16[32,256,256]{2,1,0:T(8,128)(2,1)} %param.17, s32[1024]{0:T(1024)S(1)} %pad_clamp_fusion), kind=kCustom, calls=%fused_computation.clone | custom fusion | bytes 8388736 | tf_op jit(solution)/shard_map/jit(_take)/gather | solution.py:142
  54.2 5.0 %gather_fusion.1 = bf16[32,256,256]{2,1,0:T(8,128)(2,1)} fusion(bf16[32,256,256]{2,1,0:T(8,128)(2,1)} %param.18, s32[1024]{0:T(1024)S(1)} %pad_clamp_fusion), kind=kCustom, calls=%fused_computation.1.clone | custom fusion | bytes 8388736 | tf_op jit(solution)/shard_map/jit(_take)/gather | solution.py:143
  59.2 5.9 %all-to-all-start.1 = ((bf16[8,4,2048]{2,1,0:T(4,128)(2,1)}), bf16[8,4,2048]{2,1,0:T(4,128)(2,1)S(1)}, u32[]{:S(2)}, u32[]{:S(2)}) async-start(bf16[8,4,2048]{2,1,0:T(4,128)(2,1)} %reshape.124), calls=%async_computation.1 | async-start | bytes 262144 | tf_op jit(solution)/shard_map/all_to_all | solution.py:125
  65.1 5.9 %select_bitcast_fusion.1 = (bf16[32,32,2,8,128]{4,3,2,1,0:T(8,128)(2,1)}, bf16[32,32,2,8,128]{4,3,2,1,0:T(8,128)(2,1)}) fusion(bf16[32,256,256]{2,1,0:T(8,128)(2,1)} %gather_fusion, pred[32]{0:T(512)(128)(4,1)S(1)} %compare_and_fusion, bf16[32,256,256]{2,1,0:T(8,128)(2,1)} %gather_fusion.1), kind=kLoop, calls=%fused_computation.9 | loop fusion | flops 4194304 | bytes 16777248
  72.7 3.6 %fusion.43 = (f32[32,2,8]{2,1,0:T(2,128)S(1)}, f32[32,2,8,256]{3,2,1,0:T(8,128)S(1)}) fusion(bf16[32,2,8,128]{3,2,1,0:T(8,128)(2,1)S(1)} %reshape_reshape.10, bf16[32,32,2,8,128]{4,3,2,1,0:T(8,128)(2,1)} %get-tuple-element.10, pred[32,256]{1,0:T(8,128)(4,1)S(1)} %iota_compare_fusion), kind=kOutput, calls=%fused_computation.64 | convolution fusion | flops 33947136 | bytes 4859904 | tf_op jit(solution)/shard_map/ngqd,njgd->ngqj/dot_general | solution.py:25
  78.2 5.9 %all-to-all-start.5 = ((bf16[8,4,2048]{2,1,0:T(4,128)(2,1)}), bf16[8,4,2048]{2,1,0:T(4,128)(2,1)S(1)}, u32[]{:S(2)}, u32[]{:S(2)}) async-start(bf16[8,4,2048]{2,1,0:T(4,128)(2,1)} %reshape_reshape.12), calls=%async_computation.5 | async-start | bytes 262144 | tf_op jit(solution)/shard_map/all_to_all | solution.py:153
  84.4 7.1 %all-to-all-done.5 = bf16[8,4,2048]{2,1,0:T(4,128)(2,1)S(1)} async-done(((bf16[8,4,2048]{2,1,0:T(4,128)(2,1)}), bf16[8,4,2048]{2,1,0:T(4,128)(2,1)S(1)}, u32[]{:S(2)}, u32[]{:S(2)}) %all-to-all-start.5) | async-done | bytes 131104 | tf_op jit(solution)/shard_map/all_to_all | solution.py:153
  91.8 31.8 %all_gather.3 = bf16[128,2048]{1,0:T(8,128)(2,1)S(1)} all-gather(bf16[16,2048]{1,0:T(8,128)(2,1)S(1)} %fusion.8), channel_id=1, replica_groups=mesh['dp'=8,'mp'=4] {'dp'}, dimensions={0}, use_global_device_ids=true | all-gather | bytes 589824 | tf_op jit(solution)/shard_map/all_gather | solution.py:167
  123.5 3.0 %convolution_convert_fusion.2 = bf16[128,1024]{1,0:T(8,128)(2,1)S(1)} fusion(bf16[128,2048]{1,0:T(8,128)(2,1)S(1)} %all_gather.3, bf16[2048,1024]{1,0:T(8,128)(2,1)} %param.21), kind=kOutput, calls=%fused_computation.17 | convolution fusion | flops 537001984 | bytes 4980736 | tf_op jit(solution)/shard_map/dot_general | solution.py:168
  126.5 10.6 %all_to_all.45 = bf16[8,16,1024]{2,1,0:T(8,128)(2,1)S(1)} all-to-all(bf16[8,16,1024]{2,1,0:T(8,128)(2,1)S(1)} %bitcast.55), channel_id=1, replica_groups=mesh['dp'=8,'mp'=4] {'dp'}, dimensions={0} | all-to-all | bytes 524288 | tf_op jit(solution)/shard_map/all_to_all | solution.py:171
  137.2 0.8 copy.33
  138.0 20.2 %reduce-scatter.2.cloned.1.call-done = f32[16,2048]{1,0:T(8,128)} async-done(((f32[16,8192]{1,0:T(8,128)}), f32[16,2048]{1,0:T(8,128)}) %reduce-scatter.2.cloned.1.call-update) | async-done | bytes 131088 | tf_op jit(solution)/shard_map/reduce_scatter | solution.py:172
  158.2 1.5 convert_element_type.84
  (50 shorter events, 9.1 us)
Async XLA Ops:
  6.5 10.5 %copy-start = (bf16[256,256]{1,0:T(8,128)(2,1)S(1)}, bf16[256,256]{1,0:T(8,128)(2,1)}, u32[]{:S(2)}) copy-start(bf16[256,256]{1,0:T(8,128)(2,1)} %param.19) | copy-start | bytes 393220
  9.7 13.8 %all-to-all-start.2 = ((s32[8,1,4]{2,1,0:T(1,128)}), s32[8,1,4]{2,1,0:T(1,128)S(1)}, u32[]{:S(2)}, u32[]{:S(2)}) async-start(s32[8,1,4]{2,1,0:T(1,128)} %bitcast.1), calls=%async_computation.2 | async-start | bytes 8192 | tf_op jit(solution)/shard_map/all_to_all | solution.py:134
  23.6 12.5 %all-to-all-start = ((s32[8,1,4]{2,1,0:T(1,128)}), s32[8,1,4]{2,1,0:T(1,128)S(1)}, u32[]{:S(2)}, u32[]{:S(2)}) async-start(s32[8,1,4]{2,1,0:T(1,128)} %bitcast), calls=%async_computation | async-start | bytes 8192 | tf_op jit(solution)/shard_map/all_to_all | solution.py:135
  36.1 9.9 %all-to-all-start.3 = ((bf16[8,4,256]{2,1,0:T(4,128)(2,1)}), bf16[8,4,256]{2,1,0:T(4,128)(2,1)S(1)}, u32[]{:S(2)}, u32[]{:S(2)}) async-start(bf16[8,4,256]{2,1,0:T(4,128)(2,1)} %reshape.126), calls=%async_computation.3 | async-start | bytes 32768 | tf_op jit(solution)/shard_map/all_to_all | solution.py:128
  45.9 13.2 %all-to-all-start.4 = ((bf16[8,4,256]{2,1,0:T(4,128)(2,1)}), bf16[8,4,256]{2,1,0:T(4,128)(2,1)S(1)}, u32[]{:S(2)}, u32[]{:S(2)}) async-start(bf16[8,4,256]{2,1,0:T(4,128)(2,1)} %reshape.128), calls=%async_computation.4 | async-start | bytes 32768 | tf_op jit(solution)/shard_map/all_to_all | solution.py:131
  59.2 13.3 %all-to-all-start.1 = ((bf16[8,4,2048]{2,1,0:T(4,128)(2,1)}), bf16[8,4,2048]{2,1,0:T(4,128)(2,1)S(1)}, u32[]{:S(2)}, u32[]{:S(2)}) async-start(bf16[8,4,2048]{2,1,0:T(4,128)(2,1)} %reshape.124), calls=%async_computation.1 | async-start | bytes 262144 | tf_op jit(solution)/shard_map/all_to_all | solution.py:125
  72.5 4.3 %copy-start.1 = (bf16[32,32,2,8,128]{4,3,2,1,0:T(8,128)(2,1)S(1)}, bf16[32,32,2,8,128]{4,3,2,1,0:T(8,128)(2,1)}, u32[]{:S(2)}) copy-start(bf16[32,32,2,8,128]{4,3,2,1,0:T(8,128)(2,1)} %get-tuple-element.11) | copy-start | bytes 12582916
  76.4 7.8 %copy-start.2 = (s32[16]{0:T(128)S(1)}, s32[16]{0:T(128)}, u32[]{:S(2)}) copy-start(s32[16]{0:T(128)} %param.22) | copy-start | bytes 196
  76.4 7.8 %copy-start.3 = (bf16[256,256]{1,0:T(8,128)(2,1)S(1)}, bf16[256,256]{1,0:T(8,128)(2,1)}, u32[]{:S(2)}) copy-start(bf16[256,256]{1,0:T(8,128)(2,1)} %param.20) | copy-start | bytes 393220
  78.2 13.3 %all-to-all-start.5 = ((bf16[8,4,2048]{2,1,0:T(4,128)(2,1)}), bf16[8,4,2048]{2,1,0:T(4,128)(2,1)S(1)}, u32[]{:S(2)}, u32[]{:S(2)}) async-start(bf16[8,4,2048]{2,1,0:T(4,128)(2,1)} %reshape_reshape.12), calls=%async_computation.5 | async-start | bytes 262144 | tf_op jit(solution)/shard_map/all_to_all | solution.py:153
  84.2 74.0 %reduce-scatter.2.cloned.1.call-start = ((), (), s32[]{:S(2)}) async-start(), calls=%async_computation.8 | async-start | bytes 655360 | tf_op jit(solution)/shard_map/reduce_scatter | solution.py:172
Sparse Core Ops, SparseCore 0:
  138.1 20.0 reduce-scatter.1
where the time goes:
time: 167 us
  blocking collectives  42.4 us (25%)
  waiting for transfers between devices  40.2 us (24%)
  starting transfers between devices  31.9 us (19%)
  local copies, waits for them, and re-layouts  15.6 us (9%)
  between operations  13.6 us (8%)
  matrix products  11.8 us (7%)
  other arithmetic  11.1 us (7%)
    all_gather x1, blocking collectives, on_device(): all_rows = lax.all_gather(context_rows, 'dp', axis=0, tiled=True)  31.8 us
    reduce_scatter x1, waiting for transfers between devices, on_device(): lax.psum_scatter(own_rows.astype(jnp.float32), 'mp', scatter_dimension=1,...  20.2 us
    all_to_all x1, blocking collectives, on_device(): lax.all_to_all(partial_value, 'dp', split_axis=0, concat_axis=1, tiled=True)  10.6 us
    all_to_all x1, starting transfers between devices, on_device(): lax.all_to_all(pack_ints(cache_slot), 'dp', split_axis=0, concat_axis=0,...  7.31 us
    all_to_all x1, waiting for transfers between devices, on_device(): lax.all_to_all(answered, 'dp', split_axis=0, concat_axis=0, tiled=True)  7.08 us
    all_to_all x1, waiting for transfers between devices, on_device(): lax.all_to_all(pack_rows(incoming_key), 'dp', split_axis=0, concat_axis=0...  6.5 us
    all_to_all x1, waiting for transfers between devices, on_device(): lax.all_to_all(pack_ints(cached_length), 'dp', split_axis=0, concat_axis=...  6.39 us
    all_to_all x1, starting transfers between devices, on_device(): lax.all_to_all(pack_ints(cached_length), 'dp', split_axis=0, concat_axis=...  5.99 us
  transfers between devices with their start and end apart: 7, of which 5 were waited for; matrix products, arithmetic and copies ran while one was open for 14% of the time, Pallas kernels for 0%

commit v1 on v0

--- a/solution.py
+++ b/solution.py
@@ -164,7 +164,12 @@
         .astype(jnp.bfloat16)
         .reshape(row_count, head_width)
     )
-    all_rows = lax.all_gather(context_rows, "dp", axis=0, tiled=True)
+    ring = [context_rows]
+    for hop in range(7):
+        ring.append(lax.ppermute(ring[-1], "dp", [(dev, (dev + 1) % 8) for dev in range(8)]))
+    all_rows = jnp.roll(
+        jnp.concatenate(ring[::-1], axis=0), (lax.axis_index("dp") + 1) * ring[0].shape[0], axis=0
+    )
     partial_value = jnp.dot(all_rows, out_weight, preferred_element_type=jnp.float32).astype(
         jnp.bfloat16
     )

time: 167 us -> 185 us (1.11)
  waiting for transfers between devices: 40.2 us -> 89.5 us
  blocking collectives: 42.4 us -> 10.6 us
    ppermute x0 -> x7, waiting for transfers between devices: none -> 49.3 us  [on_device(): lax.ppermute(ring[-1], 'dp', [(dev, (dev + 1) % 8) for dev in range(8)])]
    all_gather x1 -> x0, blocking collectives: 31.8 us -> none  [on_device(): all_rows = lax.all_gather(context_rows, 'dp', axis=0, tiled=True)]
  transfers between devices with their start and end apart: 7 -> 14, of which waited for: 5 -> 12; matrix products, arithmetic and copies ran while one was open for 14% -> 13% of each run, Pallas kernels for 0% -> 0%
where the time goes in v1:
time: 185 us
  waiting for transfers between devices  89.5 us (48%)
  starting transfers between devices  32.1 us (17%)
  local copies, waits for them, and re-layouts  15.7 us (8%)
  between operations  13.7 us (7%)
  matrix products  11.8 us (6%)
  other arithmetic  11.1 us (6%)
  blocking collectives  10.6 us (6%)
    ppermute x7, waiting for transfers between devices, on_device(): lax.ppermute(ring[-1], 'dp', [(dev, (dev + 1) % 8) for dev in range(8)])  49.3 us
    reduce_scatter x1, waiting for transfers between devices, on_device(): lax.psum_scatter(own_rows.astype(jnp.float32), 'mp', scatter_dimension=1,...  20.1 us
    all_to_all x1, blocking collectives, on_device(): lax.all_to_all(partial_value, 'dp', split_axis=0, concat_axis=1, tiled=True)  10.6 us
    all_to_all x1, starting transfers between devices, on_device(): lax.all_to_all(pack_ints(cache_slot), 'dp', split_axis=0, concat_axis=0,...  7.31 us
    all_to_all x1, waiting for transfers between devices, on_device(): lax.all_to_all(answered, 'dp', split_axis=0, concat_axis=0, tiled=True)  7.08 us
    all_to_all x1, waiting for transfers between devices, on_device(): lax.all_to_all(pack_rows(incoming_key), 'dp', split_axis=0, concat_axis=0...  6.5 us
    all_to_all x1, waiting for transfers between devices, on_device(): lax.all_to_all(pack_ints(cached_length), 'dp', split_axis=0, concat_axis=...  6.38 us
    all_to_all x1, starting transfers between devices, on_device(): lax.all_to_all(pack_ints(cached_length), 'dp', split_axis=0, concat_axis=...  5.99 us
  transfers between devices with their start and end apart: 14, of which 12 were waited for; matrix products, arithmetic and copies ran while one was open for 13% of the time, Pallas kernels for 0%

profile of v1, /device:TPU:0, one launch (start us, length us, event | category | flops | bytes accessed | tf_op | source)
XLA Modules:
  0.0 184.5 jit_solution(9260752460962706999)
XLA Ops:
  9.7 7.3 %all-to-all-start.2 = ((s32[8,1,4]{2,1,0:T(1,128)}), s32[8,1,4]{2,1,0:T(1,128)S(1)}, u32[]{:S(2)}, u32[]{:S(2)}) async-start(s32[8,1,4]{2,1,0:T(1,128)} %bitcast.1), calls=%async_computation.2 | async-start | bytes 8192 | tf_op jit(solution)/shard_map/all_to_all | solution.py:134
  23.6 6.0 %all-to-all-start = ((s32[8,1,4]{2,1,0:T(1,128)}), s32[8,1,4]{2,1,0:T(1,128)S(1)}, u32[]{:S(2)}, u32[]{:S(2)}) async-start(s32[8,1,4]{2,1,0:T(1,128)} %bitcast), calls=%async_computation | async-start | bytes 8192 | tf_op jit(solution)/shard_map/all_to_all | solution.py:135
  29.7 6.4 %all-to-all-done = s32[8,1,4]{2,1,0:T(1,128)S(1)} async-done(((s32[8,1,4]{2,1,0:T(1,128)}), s32[8,1,4]{2,1,0:T(1,128)S(1)}, u32[]{:S(2)}, u32[]{:S(2)}) %all-to-all-start) | async-done | bytes 160 | tf_op jit(solution)/shard_map/all_to_all | solution.py:135
  36.1 3.3 %all-to-all-start.3 = ((bf16[8,4,256]{2,1,0:T(4,128)(2,1)}), bf16[8,4,256]{2,1,0:T(4,128)(2,1)S(1)}, u32[]{:S(2)}, u32[]{:S(2)}) async-start(bf16[8,4,256]{2,1,0:T(4,128)(2,1)} %reshape.126), calls=%async_computation.3 | async-start | bytes 32768 | tf_op jit(solution)/shard_map/all_to_all | solution.py:128
  39.4 6.5 %all-to-all-done.3 = bf16[8,4,256]{2,1,0:T(4,128)(2,1)S(1)} async-done(((bf16[8,4,256]{2,1,0:T(4,128)(2,1)}), bf16[8,4,256]{2,1,0:T(4,128)(2,1)S(1)}, u32[]{:S(2)}, u32[]{:S(2)}) %all-to-all-start.3) | async-done | bytes 16416 | tf_op jit(solution)/shard_map/all_to_all | solution.py:128
  45.9 3.3 %all-to-all-start.4 = ((bf16[8,4,256]{2,1,0:T(4,128)(2,1)}), bf16[8,4,256]{2,1,0:T(4,128)(2,1)S(1)}, u32[]{:S(2)}, u32[]{:S(2)}) async-start(bf16[8,4,256]{2,1,0:T(4,128)(2,1)} %reshape.128), calls=%async_computation.4 | async-start | bytes 32768 | tf_op jit(solution)/shard_map/all_to_all | solution.py:131
  49.3 4.9 %gather_fusion = bf16[32,256,256]{2,1,0:T(8,128)(2,1)} fusion(bf16[32,256,256]{2,1,0:T(8,128)(2,1)} %param.17, s32[1024]{0:T(1024)S(1)} %pad_clamp_fusion), kind=kCustom, calls=%fused_computation.clone | custom fusion | bytes 8388736 | tf_op jit(solution)/shard_map/jit(_take)/gather | solution.py:142
  54.2 5.0 %gather_fusion.1 = bf16[32,256,256]{2,1,0:T(8,128)(2,1)} fusion(bf16[32,256,256]{2,1,0:T(8,128)(2,1)} %param.18, s32[1024]{0:T(1024)S(1)} %pad_clamp_fusion), kind=kCustom, calls=%fused_computation.1.clone | custom fusion | bytes 8388736 | tf_op jit(solution)/shard_map/jit(_take)/gather | solution.py:143
  59.2 5.9 %all-to-all-start.1 = ((bf16[8,4,2048]{2,1,0:T(4,128)(2,1)}), bf16[8,4,2048]{2,1,0:T(4,128)(2,1)S(1)}, u32[]{:S(2)}, u32[]{:S(2)}) async-start(bf16[8,4,2048]{2,1,0:T(4,128)(2,1)} %reshape.124), calls=%async_computation.1 | async-start | bytes 262144 | tf_op jit(solution)/shard_map/all_to_all | solution.py:125
  65.1 5.9 %select_bitcast_fusion.1 = (bf16[32,32,2,8,128]{4,3,2,1,0:T(8,128)(2,1)}, bf16[32,32,2,8,128]{4,3,2,1,0:T(8,128)(2,1)}) fusion(bf16[32,256,256]{2,1,0:T(8,128)(2,1)} %gather_fusion, pred[32]{0:T(512)(128)(4,1)S(1)} %compare_and_fusion, bf16[32,256,256]{2,1,0:T(8,128)(2,1)} %gather_fusion.1), kind=kLoop, calls=%fused_computation.9 | loop fusion | flops 4194304 | bytes 16777248
  72.7 3.6 %fusion.45 = (f32[32,2,8]{2,1,0:T(2,128)S(1)}, f32[32,2,8,256]{3,2,1,0:T(8,128)S(1)}) fusion(bf16[32,2,8,128]{3,2,1,0:T(8,128)(2,1)S(1)} %reshape_reshape.10, bf16[32,32,2,8,128]{4,3,2,1,0:T(8,128)(2,1)} %get-tuple-element.10, pred[32,256]{1,0:T(8,128)(4,1)S(1)} %iota_compare_fusion), kind=kOutput, calls=%fused_computation.82 | convolution fusion | flops 33947136 | bytes 4859904 | tf_op jit(solution)/shard_map/ngqd,njgd->ngqj/dot_general | solution.py:25
  78.3 5.9 %all-to-all-start.5 = ((bf16[8,4,2048]{2,1,0:T(4,128)(2,1)}), bf16[8,4,2048]{2,1,0:T(4,128)(2,1)S(1)}, u32[]{:S(2)}, u32[]{:S(2)}) async-start(bf16[8,4,2048]{2,1,0:T(4,128)(2,1)} %reshape_reshape.12), calls=%async_computation.5 | async-start | bytes 262144 | tf_op jit(solution)/shard_map/all_to_all | solution.py:153
  84.4 7.1 %all-to-all-done.5 = bf16[8,4,2048]{2,1,0:T(4,128)(2,1)S(1)} async-done(((bf16[8,4,2048]{2,1,0:T(4,128)(2,1)}), bf16[8,4,2048]{2,1,0:T(4,128)(2,1)S(1)}, u32[]{:S(2)}, u32[]{:S(2)}) %all-to-all-start.5) | async-done | bytes 131104 | tf_op jit(solution)/shard_map/all_to_all | solution.py:153
  92.0 6.9 %collective-permute-done = bf16[16,2048]{1,0:T(8,128)(2,1)S(1)} collective-permute-done((bf16[16,2048]{1,0:T(8,128)(2,1)S(1)}, bf16[16,2048]{1,0:T(8,128)(2,1)S(1)}, u32[]{:S(2)}, u32[]{:S(2)}) %collective-permute-start) | collective-permute-done | bytes 65568 | tf_op jit(solution)/shard_map/ppermute | solution.py:169
  98.9 7.0 %collective-permute-done.1 = bf16[16,2048]{1,0:T(8,128)(2,1)S(1)} collective-permute-done((bf16[16,2048]{1,0:T(8,128)(2,1)S(1)}, bf16[16,2048]{1,0:T(8,128)(2,1)S(1)}, u32[]{:S(2)}, u32[]{:S(2)}) %collective-permute-start.1) | collective-permute-done | bytes 65568 | tf_op jit(solution)/shard_map/ppermute | solution.py:169
  105.9 7.0 %collective-permute-done.2 = bf16[16,2048]{1,0:T(8,128)(2,1)S(1)} collective-permute-done((bf16[16,2048]{1,0:T(8,128)(2,1)S(1)}, bf16[16,2048]{1,0:T(8,128)(2,1)S(1)}, u32[]{:S(2)}, u32[]{:S(2)}) %collective-permute-start.2) | collective-permute-done | bytes 65568 | tf_op jit(solution)/shard_map/ppermute | solution.py:169
  112.8 7.0 %collective-permute-done.3 = bf16[16,2048]{1,0:T(8,128)(2,1)S(1)} collective-permute-done((bf16[16,2048]{1,0:T(8,128)(2,1)S(1)}, bf16[16,2048]{1,0:T(8,128)(2,1)S(1)}, u32[]{:S(2)}, u32[]{:S(2)}) %collective-permute-start.3) | collective-permute-done | bytes 65568 | tf_op jit(solution)/shard_map/ppermute | solution.py:169
  119.8 7.0 %collective-permute-done.4 = bf16[16,2048]{1,0:T(8,128)(2,1)S(1)} collective-permute-done((bf16[16,2048]{1,0:T(8,128)(2,1)S(1)}, bf16[16,2048]{1,0:T(8,128)(2,1)S(1)}, u32[]{:S(2)}, u32[]{:S(2)}) %collective-permute-start.4) | collective-permute-done | bytes 65568 | tf_op jit(solution)/shard_map/ppermute | solution.py:169
  126.8 7.0 %collective-permute-done.5 = bf16[16,2048]{1,0:T(8,128)(2,1)S(1)} collective-permute-done((bf16[16,2048]{1,0:T(8,128)(2,1)S(1)}, bf16[16,2048]{1,0:T(8,128)(2,1)S(1)}, u32[]{:S(2)}, u32[]{:S(2)}) %collective-permute-start.5) | collective-permute-done | bytes 65568 | tf_op jit(solution)/shard_map/ppermute | solution.py:169
  133.7 7.6 %collective-permute-done.6 = bf16[16,2048]{1,0:T(8,128)(2,1)S(1)} collective-permute-done((bf16[16,2048]{1,0:T(8,128)(2,1)S(1)}, bf16[16,2048]{1,0:T(8,128)(2,1)S(1)}, u32[]{:S(2)}, u32[]{:S(2)}) %collective-permute-start.6) | collective-permute-done | bytes 65568 | tf_op jit(solution)/shard_map/ppermute | solution.py:169
  141.6 2.9 %convolution_convert_fusion.2 = bf16[128,1024]{1,0:T(8,128)(2,1)S(1)} fusion(bf16[2048,1024]{1,0:T(8,128)(2,1)} %param.21, bf16[256,2048]{1,0:T(8,128)(2,1)S(1)} %constant_dynamic-update-slice_fusion, s32[]{:T(128)S(6)} %select_n.49), kind=kOutput, calls=%fused_computation.17 | convolution fusion | flops 537001984 | bytes 4980740 | tf_op jit(solution)/shard_map/dot_general | solution.py:173
  144.5 10.6 %all_to_all.45 = bf16[8,16,1024]{2,1,0:T(8,128)(2,1)S(1)} all-to-all(bf16[8,16,1024]{2,1,0:T(8,128)(2,1)S(1)} %bitcast.54), channel_id=1, replica_groups=mesh['dp'=8,'mp'=4] {'dp'}, dimensions={0} | all-to-all | bytes 524288 | tf_op jit(solution)/shard_map/all_to_all | solution.py:176
  156.1 20.1 %reduce-scatter.2.cloned.1.call-done = f32[16,2048]{1,0:T(8,128)} async-done(((f32[16,8192]{1,0:T(8,128)}), f32[16,2048]{1,0:T(8,128)}) %reduce-scatter.2.cloned.1.call-update) | async-done | bytes 131088 | tf_op jit(solution)/shard_map/reduce_scatter | solution.py:177
  176.1 1.5 convert_element_type.84
  (79 shorter events, 15.2 us)
Async XLA Ops:
  6.5 10.5 %copy-start = (bf16[256,256]{1,0:T(8,128)(2,1)S(1)}, bf16[256,256]{1,0:T(8,128)(2,1)}, u32[]{:S(2)}) copy-start(bf16[256,256]{1,0:T(8,128)(2,1)} %param.19) | copy-start | bytes 393220
  9.7 13.8 %all-to-all-start.2 = ((s32[8,1,4]{2,1,0:T(1,128)}), s32[8,1,4]{2,1,0:T(1,128)S(1)}, u32[]{:S(2)}, u32[]{:S(2)}) async-start(s32[8,1,4]{2,1,0:T(1,128)} %bitcast.1), calls=%async_computation.2 | async-start | bytes 8192 | tf_op jit(solution)/shard_map/all_to_all | solution.py:134
  23.6 12.5 %all-to-all-start = ((s32[8,1,4]{2,1,0:T(1,128)}), s32[8,1,4]{2,1,0:T(1,128)S(1)}, u32[]{:S(2)}, u32[]{:S(2)}) async-start(s32[8,1,4]{2,1,0:T(1,128)} %bitcast), calls=%async_computation | async-start | bytes 8192 | tf_op jit(solution)/shard_map/all_to_all | solution.py:135
  36.1 9.9 %all-to-all-start.3 = ((bf16[8,4,256]{2,1,0:T(4,128)(2,1)}), bf16[8,4,256]{2,1,0:T(4,128)(2,1)S(1)}, u32[]{:S(2)}, u32[]{:S(2)}) async-start(bf16[8,4,256]{2,1,0:T(4,128)(2,1)} %reshape.126), calls=%async_computation.3 | async-start | bytes 32768 | tf_op jit(solution)/shard_map/all_to_all | solution.py:128
  45.9 13.3 %all-to-all-start.4 = ((bf16[8,4,256]{2,1,0:T(4,128)(2,1)}), bf16[8,4,256]{2,1,0:T(4,128)(2,1)S(1)}, u32[]{:S(2)}, u32[]{:S(2)}) async-start(bf16[8,4,256]{2,1,0:T(4,128)(2,1)} %reshape.128), calls=%async_computation.4 | async-start | bytes 32768 | tf_op jit(solution)/shard_map/all_to_all | solution.py:131
  59.2 13.3 %all-to-all-start.1 = ((bf16[8,4,2048]{2,1,0:T(4,128)(2,1)}), bf16[8,4,2048]{2,1,0:T(4,128)(2,1)S(1)}, u32[]{:S(2)}, u32[]{:S(2)}) async-start(bf16[8,4,2048]{2,1,0:T(4,128)(2,1)} %reshape.124), calls=%async_computation.1 | async-start | bytes 262144 | tf_op jit(solution)/shard_map/all_to_all | solution.py:125
  72.5 4.3 %copy-start.1 = (bf16[32,32,2,8,128]{4,3,2,1,0:T(8,128)(2,1)S(1)}, bf16[32,32,2,8,128]{4,3,2,1,0:T(8,128)(2,1)}, u32[]{:S(2)}) copy-start(bf16[32,32,2,8,128]{4,3,2,1,0:T(8,128)(2,1)} %get-tuple-element.11) | copy-start | bytes 12582916
  76.4 7.8 %copy-start.2 = (s32[16]{0:T(128)S(1)}, s32[16]{0:T(128)}, u32[]{:S(2)}) copy-start(s32[16]{0:T(128)} %param.22) | copy-start | bytes 196
  76.4 7.8 %copy-start.3 = (bf16[256,256]{1,0:T(8,128)(2,1)S(1)}, bf16[256,256]{1,0:T(8,128)(2,1)}, u32[]{:S(2)}) copy-start(bf16[256,256]{1,0:T(8,128)(2,1)} %param.20) | copy-start | bytes 393220
  78.3 13.2 %all-to-all-start.5 = ((bf16[8,4,2048]{2,1,0:T(4,128)(2,1)}), bf16[8,4,2048]{2,1,0:T(4,128)(2,1)S(1)}, u32[]{:S(2)}, u32[]{:S(2)}) async-start(bf16[8,4,2048]{2,1,0:T(4,128)(2,1)} %reshape_reshape.12), calls=%async_computation.5 | async-start | bytes 262144 | tf_op jit(solution)/shard_map/all_to_all | solution.py:153
  84.2 92.0 %reduce-scatter.2.cloned.1.call-start = ((), (), s32[]{:S(2)}) async-start(), calls=%async_computation.8 | async-start | bytes 655360 | tf_op jit(solution)/shard_map/reduce_scatter | solution.py:177
  91.8 7.1 %collective-permute-start = (bf16[16,2048]{1,0:T(8,128)(2,1)S(1)}, bf16[16,2048]{1,0:T(8,128)(2,1)S(1)}, u32[]{:S(2)}, u32[]{:S(2)}) collective-permute-start(bf16[16,2048]{1,0:T(8,128)(2,1)S(1)} %fusion.8), channel_id=1, source_target_pairs={{0,4},{4,8},{8,12},{12,16},{16,20},{20,24},{24,28},{28,0},{1,5},{5... | collective-permute-start | bytes 196616 | tf_op jit(solution)/shard_map/ppermute | solution.py:169
  98.9 7.0 %collective-permute-start.1 = (bf16[16,2048]{1,0:T(8,128)(2,1)S(1)}, bf16[16,2048]{1,0:T(8,128)(2,1)S(1)}, u32[]{:S(2)}, u32[]{:S(2)}) collective-permute-start(bf16[16,2048]{1,0:T(8,128)(2,1)S(1)} %collective-permute-done), channel_id=1, source_target_pairs={{0,4},{4,8},{8,12},{12,16},{16,20},{20,24},{24,28},{28,0},{1,5},{5... | collective-permute-start | bytes 196616 | tf_op jit(solution)/shard_map/ppermute | solution.py:169
  105.9 7.0 %collective-permute-start.2 = (bf16[16,2048]{1,0:T(8,128)(2,1)S(1)}, bf16[16,2048]{1,0:T(8,128)(2,1)S(1)}, u32[]{:S(2)}, u32[]{:S(2)}) collective-permute-start(bf16[16,2048]{1,0:T(8,128)(2,1)S(1)} %collective-permute-done.1), channel_id=1, source_target_pairs={{0,4},{4,8},{8,12},{12,16},{16,20},{20,24},{24,28},{28,0},{1,5},{5... | collective-permute-start | bytes 196616 | tf_op jit(solution)/shard_map/ppermute | solution.py:169
  112.8 7.0 %collective-permute-start.3 = (bf16[16,2048]{1,0:T(8,128)(2,1)S(1)}, bf16[16,2048]{1,0:T(8,128)(2,1)S(1)}, u32[]{:S(2)}, u32[]{:S(2)}) collective-permute-start(bf16[16,2048]{1,0:T(8,128)(2,1)S(1)} %collective-permute-done.2), channel_id=1, source_target_pairs={{0,4},{4,8},{8,12},{12,16},{16,20},{20,24},{24,28},{28,0},{1,5},{5... | collective-permute-start | bytes 196616 | tf_op jit(solution)/shard_map/ppermute | solution.py:169
  119.8 7.0 %collective-permute-start.4 = (bf16[16,2048]{1,0:T(8,128)(2,1)S(1)}, bf16[16,2048]{1,0:T(8,128)(2,1)S(1)}, u32[]{:S(2)}, u32[]{:S(2)}) collective-permute-start(bf16[16,2048]{1,0:T(8,128)(2,1)S(1)} %collective-permute-done.3), channel_id=1, source_target_pairs={{0,4},{4,8},{8,12},{12,16},{16,20},{20,24},{24,28},{28,0},{1,5},{5... | collective-permute-start | bytes 196616 | tf_op jit(solution)/shard_map/ppermute | solution.py:169
  126.8 7.0 %collective-permute-start.5 = (bf16[16,2048]{1,0:T(8,128)(2,1)S(1)}, bf16[16,2048]{1,0:T(8,128)(2,1)S(1)}, u32[]{:S(2)}, u32[]{:S(2)}) collective-permute-start(bf16[16,2048]{1,0:T(8,128)(2,1)S(1)} %collective-permute-done.4), channel_id=1, source_target_pairs={{0,4},{4,8},{8,12},{12,16},{16,20},{20,24},{24,28},{28,0},{1,5},{5... | collective-permute-start | bytes 196616 | tf_op jit(solution)/shard_map/ppermute | solution.py:169
  133.7 7.6 %collective-permute-start.6 = (bf16[16,2048]{1,0:T(8,128)(2,1)S(1)}, bf16[16,2048]{1,0:T(8,128)(2,1)S(1)}, u32[]{:S(2)}, u32[]{:S(2)}) collective-permute-start(bf16[16,2048]{1,0:T(8,128)(2,1)S(1)} %collective-permute-done.5), channel_id=1, source_target_pairs={{0,4},{4,8},{8,12},{12,16},{16,20},{20,24},{24,28},{28,0},{1,5},{5... | collective-permute-start | bytes 196616 | tf_op jit(solution)/shard_map/ppermute | solution.py:169
Sparse Core Ops, SparseCore 0:
  156.2 19.9 reduce-scatter.1
